TPU v7x, 256 devices: a whole 4x4x8 slice. The times are simulated.
256 devices in a mesh: row: 16 (over y_hi, z), col: 16 (over x, y_lo, core).
Axes of the slice: x: 4, y: 4 (y_hi: 2, y_lo: 2; y = y_hi * 2 + y_lo), z: 8, core: 2. Of those that a mesh axis runs over, the one named last changes fastest.
Arguments:
- fields: float32 [1, 4, 256, 256, 256], P(None, None, 'row', 'col'), may hold values from -6 to 6
- cotangent: float32 [1, 4, 256, 256, 256], P(None, None, 'row', 'col'), may hold values from -6 to 6
- spec_weights: float32 [2, 4, 4, 16, 16, 16], replicated, may hold values from -96 to 96
- point_weights: float32 [4, 4], replicated, may hold values from -3 to 3
- bias: float32 [4], replicated, may hold values from -3 to 3
Outputs:
- grad_fields: float32 [1, 4, 256, 256, 256], P(None, None, 'row', 'col')
- grad_spectral: float32 [2, 4, 4, 16, 16, 16], replicated
All inputs are finite; a program needn't handle non-finite values.
Results may differ from a plain program's by a relative error of at most 0.00011.
Values sent between devices are 32-bit elements; how exact they have to be, the bound alone decides.
A program may use at most 64 MiB of HBM per device.

v0:
```python
import math
import jax
import jax.numpy as jnp
from jax import lax
from jax.sharding import PartitionSpec as P

C = 4
NX = 256
NY = 256
NZ = 256
MX = 16
MY = 16
MZ = 16
highest = lax.Precision.HIGHEST


def phase_tables(number, length, signed, start, count):
    wavenum = jnp.arange(number, dtype=jnp.int32)
    if signed:
        wavenum = jnp.where(wavenum < number // 2, wavenum, wavenum + length - number)
    points = start + jnp.arange(count, dtype=jnp.int32)
    angles = (
        2.0 * math.pi / length * (points[:, None] * wavenum[None, :] % length).astype(jnp.float32)
    )
    return (jnp.cos(angles), jnp.sin(angles))


def forward_table(number, length, start, count):
    cosine, sine = phase_tables(number, length, True, start, count)
    return jnp.stack([jnp.stack([cosine, -sine], 1), jnp.stack([sine, cosine], 1)], 0)


def inverse_table(number, length, start, count):
    cosine, sine = phase_tables(number, length, True, start, count)
    cosine = cosine.T
    sine = sine.T
    return jnp.stack([jnp.stack([cosine, sine], 1), jnp.stack([-sine, cosine], 1)], 0)


def first_table():
    cos_x, sin_x = phase_tables(MX, NX, False, 0, NX)
    return jnp.stack([cos_x, -sin_x], 1)


def last_table():
    cos_x, sin_x = phase_tables(MX, NX, False, 0, NX)
    wavenum = jnp.arange(MX, dtype=jnp.int32)
    weighting = jnp.where(wavenum == 0, 1.0, 2.0).astype(jnp.float32) / float(NX * NY * NZ)
    return jnp.stack([cos_x.T * weighting[:, None], -sin_x.T * weighting[:, None]], 0)


def to_modes(field):
    along_x = jnp.einsum("bcyzx,xtp->btpczy", field, first_table(), precision=highest)
    gathered = lax.all_to_all(along_x, "row", split_axis=2, concat_axis=5, tiled=True)
    along_y = jnp.einsum(
        "bspczy,sytq->btpcqz", gathered, forward_table(MY, NY, 0, NY), precision=highest
    )
    swapped = lax.all_to_all(along_y, "col", split_axis=4, concat_axis=5, tiled=True)
    return jnp.einsum(
        "bspcqz,sztr->btpcqr", swapped, forward_table(MZ, NZ, 0, NZ), precision=highest
    )


def from_modes(modes):
    along_z = jnp.einsum(
        "bspcqr,srtz->btpcqz", modes, inverse_table(MZ, NZ, 0, NZ), precision=highest
    )
    swapped = lax.all_to_all(along_z, "col", split_axis=5, concat_axis=4, tiled=True)
    along_y = jnp.einsum(
        "bspcqz,sqty->btpczy", swapped, inverse_table(MY, NY, 0, NY), precision=highest
    )
    gathered = lax.all_to_all(along_y, "row", split_axis=5, concat_axis=2, tiled=True)
    return jnp.einsum("btpczy,tpx->bcyzx", gathered, last_table(), precision=highest)


def per_device(fields, cotangent, spec_weights, point_weights, bias):
    row_pos = lax.axis_index("row")
    col_pos = lax.axis_index("col")
    zero_index = jnp.zeros((), jnp.int32)
    kx_local = MX // lax.axis_size("row")
    ky_local = MY // lax.axis_size("col")
    starts = (
        zero_index,
        zero_index,
        zero_index,
        row_pos * kx_local,
        col_pos * ky_local,
        zero_index,
    )
    owned_weights = lax.dynamic_slice(spec_weights, starts, (2, C, C, kx_local, ky_local, MZ))
    kx_start = row_pos * kx_local
    weight_real = owned_weights[0]
    weight_imag = owned_weights[1]
    spectrum_u = to_modes(fields)
    input_real = spectrum_u[:, 0]
    input_imag = spectrum_u[:, 1]
    mix_form = "bpiqr,iopqr->bpoqr"
    mixed_real = jnp.einsum(mix_form, input_real, weight_real, precision=highest) - jnp.einsum(
        mix_form, input_imag, weight_imag, precision=highest
    )
    mixed_imag = jnp.einsum(mix_form, input_real, weight_imag, precision=highest) + jnp.einsum(
        mix_form, input_imag, weight_real, precision=highest
    )
    spectral_term = from_modes(jnp.stack([mixed_real, mixed_imag], 1))
    local_term = jnp.einsum("bcyzx,co->boyzx", fields, point_weights, precision=highest)
    pre_activation = spectral_term + local_term + bias[None, :, None, None, None]
    gelu_slope = 0.5 * (1.0 + lax.erf(pre_activation / math.sqrt(2.0))) + pre_activation * jnp.exp(
        -0.5 * pre_activation * pre_activation
    ) / math.sqrt(2.0 * math.pi)
    upstream = cotangent * gelu_slope
    spectrum_h = to_modes(upstream)
    back_real = spectrum_h[:, 0]
    back_imag = spectrum_h[:, 1]
    grad_form = "bpiqr,bpoqr->iopqr"
    grad_real = jnp.einsum(grad_form, input_real, back_real, precision=highest) + jnp.einsum(
        grad_form, input_imag, back_imag, precision=highest
    )
    grad_imag = jnp.einsum(grad_form, input_real, back_imag, precision=highest) - jnp.einsum(
        grad_form, input_imag, back_real, precision=highest
    )
    wave_global = kx_start + jnp.arange(kx_local, dtype=jnp.int32)
    factor = jnp.where(wave_global == 0, 1.0, 2.0).astype(jnp.float32) / float(NX * NY * NZ)
    grad_block = jnp.stack([grad_real, grad_imag], 0) * factor[None, None, None, :, None, None]
    adj_form = "iopqr,bpoqr->bpiqr"
    adjoint_real = jnp.einsum(adj_form, weight_real, back_real, precision=highest) + jnp.einsum(
        adj_form, weight_imag, back_imag, precision=highest
    )
    adjoint_imag = jnp.einsum(adj_form, weight_real, back_imag, precision=highest) - jnp.einsum(
        adj_form, weight_imag, back_real, precision=highest
    )
    grad_fields = from_modes(jnp.stack([adjoint_real, adjoint_imag], 1))
    grad_fields = grad_fields + jnp.einsum(
        "boyzx,co->bcyzx", upstream, point_weights, precision=highest
    )
    full_grad = jnp.zeros((2, C, C, MX, MY, MZ), jnp.float32)
    full_grad = lax.dynamic_update_slice(full_grad, grad_block, starts)
    grad_spectral = lax.psum(full_grad, ("row", "col"))
    return (grad_fields, grad_spectral)


def solution(mesh):
    placed = (P(None, None, "row", "col", None), P(None, None, "row", "col", None), P(), P(), P())
    return jax.shard_map(
        per_device,
        mesh=mesh,
        in_specs=placed,
        out_specs=(P(None, None, "row", "col", None), P()),
        check_vma=False,
    )
```

profile of v0, /device:TPU:2, one launch (start us, length us, event | category | flops | bytes accessed | tf_op | source)
XLA Modules:
  0.0 427.5 jit_solution(5578637302729846114)
XLA Ops:
  8.4 4.4 %convolution_bitcast_fusion.3 = f32[1,2,16,4,16,16]{4,2,5,3,1,0:T(8,128)S(1)} fusion(f32[1,4,16,16,256]{4,3,2,1,0:T(8,128)S(1)} %copy-done, f32[256,1,16]{0,2,1:T(8,128)S(1)} %get-tuple-element.46, f32[256,1,16]{0,2,1:T(8,128)S(1)} %get-tuple-element.47), kind=kOutput, calls=%fused_computation.7 | convolution fusion | flops 100671488 | bytes 1212416 | tf_op jit(solution)/shard_map/bcyzx,xtp->btpczy/dot_general | solution.py:53
  14.2 11.2 %all-to-all-start = ((f32[16,1,2048]{2,1,0:T(1,128)}), f32[16,1,2048]{2,1,0:T(1,128)S(1)}, u32[]{:S(2)}, u32[]{:S(2)}) async-start(f32[16,1,2048]{2,1,0:T(1,128)} %reshape.708), calls=%async_computation | async-start | bytes 262144 | tf_op jit(solution)/shard_map/all_to_all | solution.py:54
  25.8 9.7 %all-to-all-done = f32[16,1,2048]{2,1,0:T(1,128)S(1)} async-done(((f32[16,1,2048]{2,1,0:T(1,128)}), f32[16,1,2048]{2,1,0:T(1,128)S(1)}, u32[]{:S(2)}, u32[]{:S(2)}) %all-to-all-start) | async-done | bytes 131104 | tf_op jit(solution)/shard_map/all_to_all | solution.py:54
  39.8 5.0 %all-to-all-start.1 = ((f32[16,1,128]{2,1,0:T(1,128)}), f32[16,1,128]{2,1,0:T(1,128)S(1)}, u32[]{:S(2)}, u32[]{:S(2)}) async-start(f32[16,1,128]{2,1,0:T(1,128)} %reshape.710), calls=%async_computation.1 | async-start | bytes 16384 | tf_op jit(solution)/shard_map/all_to_all | solution.py:58
  45.6 3.8 all-to-all-done.1
  52.0 4.7 %all-to-all-start.2 = ((f32[16,1,128]{2,1,0:T(1,128)}), f32[16,1,128]{2,1,0:T(1,128)S(1)}, u32[]{:S(2)}, u32[]{:S(2)}) async-start(f32[16,1,128]{2,1,0:T(1,128)} %reshape.712), calls=%async_computation.2 | async-start | bytes 16384 | tf_op jit(solution)/shard_map/all_to_all | solution.py:68
  56.8 2.8 fusion.16
  59.6 1.9 all-to-all-done.2
  65.1 3.9 all-to-all-start.3
  69.1 10.0 %all-to-all-done.3 = f32[16,1,2048]{2,1,0:T(1,128)S(1)} async-done(((f32[16,1,2048]{2,1,0:T(1,128)}), f32[16,1,2048]{2,1,0:T(1,128)S(1)}, u32[]{:S(2)}, u32[]{:S(2)}) %all-to-all-start.3) | async-done | bytes 131104 | tf_op jit(solution)/shard_map/all_to_all | solution.py:72
  80.7 2.2 copy.86
  82.9 4.0 fusion.8
  86.9 4.3 convolution_bitcast_fusion.1
  91.9 13.1 %all_to_all.96 = f32[16,1,2048]{2,1,0:T(1,128)S(1)} all-to-all(f32[16,1,2048]{2,1,0:T(1,128)S(1)} %reshape.716), channel_id=1, replica_groups=mesh['row'=16,'col'=16] {'row'}, dimensions={0} | all-to-all | bytes 262144 | tf_op jit(solution)/shard_map/all_to_all | solution.py:54
  110.3 8.6 %all_to_all.97 = f32[16,1,128]{2,1,0:T(1,128)S(1)} all-to-all(f32[16,1,128]{2,1,0:T(1,128)S(1)} %reshape.718), channel_id=1, replica_groups=mesh['row'=16,'col'=16] {'col'}, dimensions={0} | all-to-all | bytes 16384 | tf_op jit(solution)/shard_map/all_to_all | solution.py:58
  121.6 4.7 %all-to-all-start.6 = ((f32[16,1,128]{2,1,0:T(1,128)}), f32[16,1,128]{2,1,0:T(1,128)S(1)}, u32[]{:S(2)}, u32[]{:S(2)}) async-start(f32[16,1,128]{2,1,0:T(1,128)} %reshape.720), calls=%async_computation.6 | async-start | bytes 16384 | tf_op jit(solution)/shard_map/all_to_all | solution.py:68
  126.3 4.7 %all-to-all-done.6 = f32[16,1,128]{2,1,0:T(1,128)S(1)} async-done(((f32[16,1,128]{2,1,0:T(1,128)}), f32[16,1,128]{2,1,0:T(1,128)S(1)}, u32[]{:S(2)}, u32[]{:S(2)}) %all-to-all-start.6) | async-done | bytes 8224 | tf_op jit(solution)/shard_map/all_to_all | solution.py:68
  134.7 3.8 all-to-all-start.7
  138.6 2.6 fusion.13
  141.2 2.5 broadcast_in_dim.14
  145.3 3.3 all-to-all-done.7
  151.3 2.2 copy.103
  156.5 259.6 %all-reduce.2.cloned.1.call-done = f32[2,4,4,16,16,16]{5,4,3,2,1,0:T(8,128)} async-done(((f32[2,4,4,16,16,16]{5,4,3,2,1,0:T(8,128)}), f32[2,4,4,16,16,16]{5,4,3,2,1,0:T(8,128)}) %all-reduce.2.cloned.1.call-update) | async-done | bytes 524304 | tf_op jit(solution)/shard_map/psum | solution.py:137
  416.0 4.7 %copy.228 = f32[2,4,4,16,16,16]{5,4,3,2,1,0:T(8,128)} copy(f32[2,4,4,16,16,16]{5,4,3,2,1,0:T(8,128)} %all-reduce.2.cloned.1.call-done) | data formatting | bytes 1048576
  (82 shorter events, 35.5 us)
Async XLA Ops:
  7.2 1.2 copy-start
  14.2 21.3 %all-to-all-start = ((f32[16,1,2048]{2,1,0:T(1,128)}), f32[16,1,2048]{2,1,0:T(1,128)S(1)}, u32[]{:S(2)}, u32[]{:S(2)}) async-start(f32[16,1,2048]{2,1,0:T(1,128)} %reshape.708), calls=%async_computation | async-start | bytes 262144 | tf_op jit(solution)/shard_map/all_to_all | solution.py:54
  36.0 20.7 %copy-start.1 = (f32[4,4]{1,0:T(4,128)S(1)}, f32[4,4]{1,0:T(4,128)}, u32[]{:S(2)}) copy-start(f32[4,4]{1,0:T(4,128)} %param.8) | copy-start | bytes 196
  39.8 9.6 %all-to-all-start.1 = ((f32[16,1,128]{2,1,0:T(1,128)}), f32[16,1,128]{2,1,0:T(1,128)S(1)}, u32[]{:S(2)}, u32[]{:S(2)}) async-start(f32[16,1,128]{2,1,0:T(1,128)} %reshape.710), calls=%async_computation.1 | async-start | bytes 16384 | tf_op jit(solution)/shard_map/all_to_all | solution.py:58
  52.0 9.5 %all-to-all-start.2 = ((f32[16,1,128]{2,1,0:T(1,128)}), f32[16,1,128]{2,1,0:T(1,128)S(1)}, u32[]{:S(2)}, u32[]{:S(2)}) async-start(f32[16,1,128]{2,1,0:T(1,128)} %reshape.712), calls=%async_computation.2 | async-start | bytes 16384 | tf_op jit(solution)/shard_map/all_to_all | solution.py:68
  56.8 26.1 %copy-start.2 = (f32[4]{0:T(128)S(1)}, f32[4]{0:T(128)}, u32[]{:S(2)}) copy-start(f32[4]{0:T(128)} %param.9) | copy-start | bytes 52
  65.1 13.9 %all-to-all-start.3 = ((f32[16,1,2048]{2,1,0:T(1,128)}), f32[16,1,2048]{2,1,0:T(1,128)S(1)}, u32[]{:S(2)}, u32[]{:S(2)}) async-start(f32[16,1,2048]{2,1,0:T(1,128)} %reshape.714), calls=%async_computation.3 | async-start | bytes 262144 | tf_op jit(solution)/shard_map/all_to_all | solution.py:72
  121.6 9.4 %all-to-all-start.6 = ((f32[16,1,128]{2,1,0:T(1,128)}), f32[16,1,128]{2,1,0:T(1,128)S(1)}, u32[]{:S(2)}, u32[]{:S(2)}) async-start(f32[16,1,128]{2,1,0:T(1,128)} %reshape.720), calls=%async_computation.6 | async-start | bytes 16384 | tf_op jit(solution)/shard_map/all_to_all | solution.py:68
  134.7 13.9 %all-to-all-start.7 = ((f32[16,1,2048]{2,1,0:T(1,128)}), f32[16,1,2048]{2,1,0:T(1,128)S(1)}, u32[]{:S(2)}, u32[]{:S(2)}) async-start(f32[16,1,2048]{2,1,0:T(1,128)} %reshape.722), calls=%async_computation.7 | async-start | bytes 262144 | tf_op jit(solution)/shard_map/all_to_all | solution.py:72
  138.5 277.5 %all-reduce.2.cloned.1.call-start = ((), (), s32[]{:S(2)}) async-start(), calls=%async_computation.8 | async-start | bytes 8388608 | tf_op jit(solution)/shard_map/psum | solution.py:137
Sparse Core Ops, SparseCore 0:
  145.4 270.5 all-reduce.1
where the time goes:
time: 428 us
  waiting for transfers between devices  293 us (68%)
  local copies, waits for them, and re-layouts  35.6 us (8%)
  starting transfers between devices  33.4 us (8%)
  matrix products  22.5 us (5%)
  blocking collectives  21.8 us (5%)
  between operations  14.5 us (3%)
  other arithmetic  6.94 us (2%)
    psum x1, waiting for transfers between devices, per_device(): grad_spectral = lax.psum(full_grad, ('row', 'col'))  260 us
    unnamed x26, local copies, waits for them, and re-layouts  18.6 us
    all_to_all x2, waiting for transfers between devices, from_modes(): lax.all_to_all(along_y, 'row', split_axis=5, concat_axis=2, tiled=True)  13.3 us
    all_to_all x1, blocking collectives, to_modes(): lax.all_to_all(along_x, 'row', split_axis=2, concat_axis=5, tiled=True)  13.1 us
    all_to_all x1, starting transfers between devices, to_modes(): lax.all_to_all(along_x, 'row', split_axis=2, concat_axis=5, tiled=True)  11.2 us
    all_to_all x1, waiting for transfers between devices, to_modes(): lax.all_to_all(along_x, 'row', split_axis=2, concat_axis=5, tiled=True)  9.72 us
    all_to_all x2, starting transfers between devices, from_modes(): lax.all_to_all(along_z, 'col', split_axis=5, concat_axis=4, tiled=True)  9.46 us
    dot_general x2, matrix products, to_modes(): jnp.einsum('bcyzx,xtp->btpczy', field, first_table(), precision=highest)  8.67 us
  transfers between devices with their start and end apart: 7, of which 7 were waited for; matrix products, arithmetic and copies ran while one was open for 4% of the time, Pallas kernels for 0%

commit v1 on v0

--- a/solution.py
+++ b/solution.py
@@ -134,7 +134,7 @@
     )
     full_grad = jnp.zeros((2, C, C, MX, MY, MZ), jnp.float32)
     full_grad = lax.dynamic_update_slice(full_grad, grad_block, starts)
-    grad_spectral = lax.psum(full_grad, ("row", "col"))
+    grad_spectral = lax.psum(lax.psum(full_grad, "col"), "row")
     return (grad_fields, grad_spectral)
 
 

time: 428 us -> 446 us (1.042)
  waiting for transfers between devices: 293 us -> 311 us
    psum x1 -> x2, waiting for transfers between devices: 260 us -> 281 us  [per_device(): grad_spectral = lax.psum(lax.psum(full_grad, 'col'), 'row')]
    all_to_all x2 -> x1, starting transfers between devices: 9.46 us -> 4.74 us  [from_modes(): lax.all_to_all(along_z, 'col', split_axis=5, concat_axis=4, tiled=True)]
    all_to_all x1 -> x2, starting transfers between devices: 4.96 us -> 9.68 us  [to_modes(): lax.all_to_all(along_y, 'col', split_axis=4, concat_axis=5, tiled=True)]
    all_to_all x2 -> x1, waiting for transfers between devices: 6.58 us -> 1.87 us  [from_modes(): lax.all_to_all(along_z, 'col', split_axis=5, concat_axis=4, tiled=True)]
    all_to_all x1 -> x2, waiting for transfers between devices: 3.75 us -> 8.41 us  [to_modes(): lax.all_to_all(along_y, 'col', split_axis=4, concat_axis=5, tiled=True)]
  transfers between devices with their start and end apart: 7 -> 8, of which waited for: 7 -> 7; matrix products, arithmetic and copies ran while one was open for 4% -> 4% of each run, Pallas kernels for 0% -> 0%
where the time goes in v1:
time: 446 us; the launch traced here: 445 us
  waiting for transfers between devices  311 us (70%)
  local copies, waits for them, and re-layouts  35.6 us (8%)
  starting transfers between devices  33.1 us (7%)
  matrix products  22.5 us (5%)
  blocking collectives  22 us (5%)
  between operations  14.5 us (3%)
  other arithmetic  6.56 us (1%)
    psum x2, waiting for transfers between devices, per_device(): grad_spectral = lax.psum(lax.psum(full_grad, 'col'), 'row')  281 us
    unnamed x26, local copies, waits for them, and re-layouts  18.6 us
    all_to_all x1, blocking collectives, to_modes(): lax.all_to_all(along_x, 'row', split_axis=2, concat_axis=5, tiled=True)  13.1 us
    all_to_all x1, starting transfers between devices, to_modes(): lax.all_to_all(along_x, 'row', split_axis=2, concat_axis=5, tiled=True)  11.2 us
    all_to_all x2, waiting for transfers between devices, from_modes(): lax.all_to_all(along_y, 'row', split_axis=5, concat_axis=2, tiled=True)  9.97 us
    all_to_all x1, waiting for transfers between devices, to_modes(): lax.all_to_all(along_x, 'row', split_axis=2, concat_axis=5, tiled=True)  9.72 us
    all_to_all x2, starting transfers between devices, to_modes(): lax.all_to_all(along_y, 'col', split_axis=4, concat_axis=5, tiled=True)  9.68 us
  transfers between devices with their start and end apart: 8, of which 7 were waited for; matrix products, arithmetic and copies ran while one was open for 4% of the time, Pallas kernels for 0%

profile of v1, /device:TPU:2, one launch (start us, length us, event | category | flops | bytes accessed | tf_op | source)
XLA Modules:
  0.0 444.9 jit_solution(5522735286655537487)
XLA Ops:
  8.4 4.4 convolution_bitcast_fusion.3
  14.2 11.2 %all-to-all-start = ((f32[16,1,2048]{2,1,0:T(1,128)}), f32[16,1,2048]{2,1,0:T(1,128)S(1)}, u32[]{:S(2)}, u32[]{:S(2)}) async-start(f32[16,1,2048]{2,1,0:T(1,128)} %reshape.708), calls=%async_computation | async-start | bytes 262144 | tf_op jit(solution)/shard_map/all_to_all | solution.py:54
  25.8 9.7 %all-to-all-done = f32[16,1,2048]{2,1,0:T(1,128)S(1)} async-done(((f32[16,1,2048]{2,1,0:T(1,128)}), f32[16,1,2048]{2,1,0:T(1,128)S(1)}, u32[]{:S(2)}, u32[]{:S(2)}) %all-to-all-start) | async-done | bytes 131104 | tf_op jit(solution)/shard_map/all_to_all | solution.py:54
  39.7 5.0 %all-to-all-start.1 = ((f32[16,1,128]{2,1,0:T(1,128)}), f32[16,1,128]{2,1,0:T(1,128)S(1)}, u32[]{:S(2)}, u32[]{:S(2)}) async-start(f32[16,1,128]{2,1,0:T(1,128)} %reshape.710), calls=%async_computation.1 | async-start | bytes 16384 | tf_op jit(solution)/shard_map/all_to_all | solution.py:58
  45.5 3.8 all-to-all-done.1
  51.9 4.7 %all-to-all-start.2 = ((f32[16,1,128]{2,1,0:T(1,128)}), f32[16,1,128]{2,1,0:T(1,128)S(1)}, u32[]{:S(2)}, u32[]{:S(2)}) async-start(f32[16,1,128]{2,1,0:T(1,128)} %reshape.712), calls=%async_computation.2 | async-start | bytes 16384 | tf_op jit(solution)/shard_map/all_to_all | solution.py:68
  56.6 2.8 fusion.16
  59.4 1.9 all-to-all-done.2
  64.9 3.9 all-to-all-start.3
  68.9 10.0 %all-to-all-done.3 = f32[16,1,2048]{2,1,0:T(1,128)S(1)} async-done(((f32[16,1,2048]{2,1,0:T(1,128)}), f32[16,1,2048]{2,1,0:T(1,128)S(1)}, u32[]{:S(2)}, u32[]{:S(2)}) %all-to-all-start.3) | async-done | bytes 131104 | tf_op jit(solution)/shard_map/all_to_all | solution.py:72
  80.5 2.2 copy.86
  82.7 4.0 fusion.8
  86.7 4.3 convolution_bitcast_fusion.1
  91.7 13.1 %all_to_all.96 = f32[16,1,2048]{2,1,0:T(1,128)S(1)} all-to-all(f32[16,1,2048]{2,1,0:T(1,128)S(1)} %reshape.716), channel_id=1, replica_groups=mesh['row'=16,'col'=16] {'row'}, dimensions={0} | all-to-all | bytes 262144 | tf_op jit(solution)/shard_map/all_to_all | solution.py:54
  110.7 4.7 %all-to-all-start.5 = ((f32[16,1,128]{2,1,0:T(1,128)}), f32[16,1,128]{2,1,0:T(1,128)S(1)}, u32[]{:S(2)}, u32[]{:S(2)}) async-start(f32[16,1,128]{2,1,0:T(1,128)} %reshape.718), calls=%async_computation.5 | async-start | bytes 16384 | tf_op jit(solution)/shard_map/all_to_all | solution.py:58
  115.4 4.7 %all-to-all-done.5 = f32[16,1,128]{2,1,0:T(1,128)S(1)} async-done(((f32[16,1,128]{2,1,0:T(1,128)}), f32[16,1,128]{2,1,0:T(1,128)S(1)}, u32[]{:S(2)}, u32[]{:S(2)}) %all-to-all-start.5) | async-done | bytes 8224 | tf_op jit(solution)/shard_map/all_to_all | solution.py:58
  121.3 2.5 broadcast_in_dim.14
  126.2 8.9 %all_to_all.97 = f32[16,1,128]{2,1,0:T(1,128)S(1)} all-to-all(f32[16,1,128]{2,1,0:T(1,128)S(1)} %reshape.720), channel_id=1, replica_groups=mesh['row'=16,'col'=16] {'col'}, dimensions={0} | all-to-all | bytes 16384 | tf_op jit(solution)/shard_map/all_to_all | solution.py:68
  138.8 3.5 all-to-all-start.7
  142.3 108.4 %all-reduce.3.cloned.1.call-done = f32[2,4,4,16,16,16]{5,4,3,2,1,0:T(8,128)} async-done(((f32[2,4,4,16,16,16]{5,4,3,2,1,0:T(8,128)}), f32[2,4,4,16,16,16]{5,4,3,2,1,0:T(8,128)}) %all-reduce.3.cloned.1.call-update) | async-done | bytes 524304 | tf_op jit(solution)/shard_map/psum | solution.py:137
  250.8 2.6 fusion.13
  255.9 2.2 copy.103
  261.1 172.3 %all-reduce.5.cloned.1.call-done = f32[2,4,4,16,16,16]{5,4,3,2,1,0:T(8,128)} async-done(((f32[2,4,4,16,16,16]{5,4,3,2,1,0:T(8,128)}), f32[2,4,4,16,16,16]{5,4,3,2,1,0:T(8,128)}) %all-reduce.5.cloned.1.call-update) | async-done | bytes 524304 | tf_op jit(solution)/shard_map/psum | solution.py:137
  433.4 4.7 %copy.229 = f32[2,4,4,16,16,16]{5,4,3,2,1,0:T(8,128)} copy(f32[2,4,4,16,16,16]{5,4,3,2,1,0:T(8,128)} %all-reduce.5.cloned.1.call-done) | data formatting | bytes 1048576
  (85 shorter events, 35.2 us)
Async XLA Ops:
  7.2 1.2 copy-start
  14.2 21.3 %all-to-all-start = ((f32[16,1,2048]{2,1,0:T(1,128)}), f32[16,1,2048]{2,1,0:T(1,128)S(1)}, u32[]{:S(2)}, u32[]{:S(2)}) async-start(f32[16,1,2048]{2,1,0:T(1,128)} %reshape.708), calls=%async_computation | async-start | bytes 262144 | tf_op jit(solution)/shard_map/all_to_all | solution.py:54
  36.0 20.6 %copy-start.1 = (f32[4,4]{1,0:T(4,128)S(1)}, f32[4,4]{1,0:T(4,128)}, u32[]{:S(2)}) copy-start(f32[4,4]{1,0:T(4,128)} %param.8) | copy-start | bytes 196
  39.7 9.6 %all-to-all-start.1 = ((f32[16,1,128]{2,1,0:T(1,128)}), f32[16,1,128]{2,1,0:T(1,128)S(1)}, u32[]{:S(2)}, u32[]{:S(2)}) async-start(f32[16,1,128]{2,1,0:T(1,128)} %reshape.710), calls=%async_computation.1 | async-start | bytes 16384 | tf_op jit(solution)/shard_map/all_to_all | solution.py:58
  51.9 9.5 %all-to-all-start.2 = ((f32[16,1,128]{2,1,0:T(1,128)}), f32[16,1,128]{2,1,0:T(1,128)S(1)}, u32[]{:S(2)}, u32[]{:S(2)}) async-start(f32[16,1,128]{2,1,0:T(1,128)} %reshape.712), calls=%async_computation.2 | async-start | bytes 16384 | tf_op jit(solution)/shard_map/all_to_all | solution.py:68
  56.6 26.0 %copy-start.2 = (f32[4]{0:T(128)S(1)}, f32[4]{0:T(128)}, u32[]{:S(2)}) copy-start(f32[4]{0:T(128)} %param.9) | copy-start | bytes 52
  64.9 13.9 %all-to-all-start.3 = ((f32[16,1,2048]{2,1,0:T(1,128)}), f32[16,1,2048]{2,1,0:T(1,128)S(1)}, u32[]{:S(2)}, u32[]{:S(2)}) async-start(f32[16,1,2048]{2,1,0:T(1,128)} %reshape.714), calls=%async_computation.3 | async-start | bytes 262144 | tf_op jit(solution)/shard_map/all_to_all | solution.py:72
  110.7 9.4 %all-to-all-start.5 = ((f32[16,1,128]{2,1,0:T(1,128)}), f32[16,1,128]{2,1,0:T(1,128)S(1)}, u32[]{:S(2)}, u32[]{:S(2)}) async-start(f32[16,1,128]{2,1,0:T(1,128)} %reshape.718), calls=%async_computation.5 | async-start | bytes 16384 | tf_op jit(solution)/shard_map/all_to_all | solution.py:58
  115.4 135.3 %all-reduce.3.cloned.1.call-start = ((), (), s32[]{:S(2)}) async-start(), calls=%async_computation.8 | async-start | bytes 8388608 | tf_op jit(solution)/shard_map/psum | solution.py:137
  138.8 114.6 %all-to-all-start.7 = ((f32[16,1,2048]{2,1,0:T(1,128)}), f32[16,1,2048]{2,1,0:T(1,128)S(1)}, u32[]{:S(2)}, u32[]{:S(2)}) async-start(f32[16,1,2048]{2,1,0:T(1,128)} %reshape.722), calls=%async_computation.7 | async-start | bytes 262144 | tf_op jit(solution)/shard_map/all_to_all | solution.py:72
  142.3 291.2 %all-reduce.5.cloned.1.call-start = ((), (), s32[]{:S(2)}) async-start(), calls=%async_computation.9 | async-start | bytes 8388608 | tf_op jit(solution)/shard_map/psum | solution.py:137
Sparse Core Ops, SparseCore 0:
  125.6 125.1 all-reduce.2
  253.4 179.9 all-reduce.4
